TPU v7x, 32 devices: a whole 2x2x4 slice. The times are simulated.
32 devices in a mesh: gx: 4 (over y, x), gy: 2 (over core), gz: 4 (over z).
Axes of the slice: x: 2, y: 2, z: 4, core: 2. Of those that a mesh axis runs over, the one named last changes fastest.
Arguments:
- rhs: float32 [3, 32, 32, 512], P(None, 'gx', 'gy', 'gz'), may hold values from -24 to 24
- conductivity: float32 [8], replicated, may hold values from 0.1 to 10
- fraction: float32 [3, 32, 32, 512], P(None, 'gx', 'gy', 'gz'), may hold values from 0.5 to 2
- region: int32 [32, 32, 512], P('gx', 'gy', 'gz'), may hold values from 0 to 7
- flags: int32 [3, 32, 32, 512], P(None, 'gx', 'gy', 'gz'), may hold values 0 or 1
Outputs:
- preconditioned: float32 [3, 32, 32, 512], P(None, 'gx', 'gy', 'gz')
All inputs are finite; a program needn't handle non-finite values. No bound on the sum of `flags` on one device may be relied on, other than what follows from the above.
Results may differ from a plain program's by a relative error of at most 0.00002.
Values sent between devices are 32-bit elements; how exact they have to be, the bound alone decides.
A program may use at most 64 MiB of HBM per device.

v0:
```python
import jax
import jax.numpy as jnp
from jax import lax
from jax.sharding import PartitionSpec as P

edge_damping = 0.8
node_damping = 0.8


def with_halo(cells, sides, width):
    for axis, dim in sides:
        count = lax.axis_size(axis)
        head = lax.slice_in_dim(cells, 0, width, axis=dim)
        tail = lax.slice_in_dim(cells, cells.shape[dim] - width, cells.shape[dim], axis=dim)
        cells = jnp.concatenate(
            [
                lax.ppermute(tail, axis, [(i, (i + 1) % count) for i in range(count)]),
                cells,
                lax.ppermute(head, axis, [((i + 1) % count, i) for i in range(count)]),
            ],
            axis=dim,
        )
    return cells


def upward(field, spatial):
    return jnp.roll(field, -1, axis=spatial)


def downward(field, spatial):
    return jnp.roll(field, 1, axis=spatial)


def forward_diff(field, spatial):
    return upward(field, spatial) - field


def backward_adjoint(field, spatial):
    return downward(field, spatial) - field


def curl_curl(stacked):
    first, second, third = (stacked[0], stacked[1], stacked[2])
    face_zero = forward_diff(third, 1) - forward_diff(second, 2)
    face_one = forward_diff(first, 2) - forward_diff(third, 0)
    face_two = forward_diff(second, 0) - forward_diff(first, 1)
    return jnp.stack(
        [
            backward_adjoint(face_one, 2) - backward_adjoint(face_two, 1),
            backward_adjoint(face_two, 0) - backward_adjoint(face_zero, 2),
            backward_adjoint(face_zero, 1) - backward_adjoint(face_one, 0),
        ]
    )


def conductance(conductivity, region):
    total = jnp.zeros(region.shape, conductivity.dtype)
    for number in range(conductivity.shape[0]):
        total = total + jnp.where(
            region == number, conductivity[number], jnp.zeros((), conductivity.dtype)
        )
    return total


def crop(array, width):
    leading = (slice(None),) * (array.ndim - 3)
    return array[leading + (slice(width, -width),) * 3]


def nodal_operator(stacked):
    result = 7.0 * stacked
    for spatial in range(3):
        result = result - (
            jnp.roll(stacked, -1, axis=spatial + 1) + jnp.roll(stacked, 1, axis=spatial + 1)
        )
    return result


def nodal_part(masked_res):
    gradient_rhs = backward_adjoint(masked_res[0], 0)
    for spatial in range(1, 3):
        gradient_rhs = gradient_rhs + backward_adjoint(masked_res[spatial], spatial)
    vector_rhs = [
        (masked_res[spatial] + downward(masked_res[spatial], spatial)) * 0.5 for spatial in range(3)
    ]
    nodal_rhs = jnp.stack([gradient_rhs] + vector_rhs)
    first_node = node_damping * nodal_rhs / 7.0
    second_node = first_node + node_damping * (nodal_rhs - nodal_operator(first_node)) / 7.0
    potential = second_node[0]
    parts = [
        forward_diff(potential, spatial)
        + (second_node[spatial + 1] + upward(second_node[spatial + 1], spatial)) * 0.5
        for spatial in range(3)
    ]
    return jnp.stack(parts)


def operator_shrunk(field, keeping, sigma):
    masked = keeping * field
    return crop(keeping * (curl_curl(masked) + sigma * masked) + (1.0 - keeping) * field, 1)


def unpack_wide(wide):
    wide_rhs = wide[0:3]
    wide_sigma = wide[3:6]
    wide_keep = (wide_sigma > 0.0).astype(wide_sigma.dtype)
    return (wide_rhs, wide_sigma, wide_keep)


def on_device(rhs, conductivity, fraction, region, flags):
    sigma = conductance(conductivity, region)[None] * fraction
    keeping = 1.0 - flags.astype(jnp.float32)
    packed = jnp.concatenate([rhs, keeping * sigma], axis=0)
    wide = with_halo(packed, (("gx", 1), ("gy", 2), ("gz", 3)), 4)
    wide_rhs, wide_sigma, wide_keep = unpack_wide(wide)
    wide_inverse = 1.0 / (wide_keep * (4.0 + wide_sigma) + (1.0 - wide_keep))
    first_iter = edge_damping * wide_inverse * wide_rhs
    applied = operator_shrunk(first_iter, wide_keep, wide_sigma)
    second_wide = crop(first_iter, 1) + edge_damping * crop(wide_inverse, 1) * (
        crop(wide_rhs, 1) - applied
    )
    inner_keep = crop(wide_keep, 2)
    residual_wide = crop(wide_rhs, 2) - operator_shrunk(
        second_wide, crop(wide_keep, 1), crop(wide_sigma, 1)
    )
    second_iter = crop(second_wide, 3)
    correction = keeping * crop(nodal_part(inner_keep * residual_wide), 2)
    return second_iter + correction


def solution(mesh):
    return jax.shard_map(
        on_device,
        mesh=mesh,
        in_specs=(
            P(None, "gx", "gy", "gz"),
            P(),
            P(None, "gx", "gy", "gz"),
            P("gx", "gy", "gz"),
            P(None, "gx", "gy", "gz"),
        ),
        out_specs=P(None, "gx", "gy", "gz"),
        check_vma=False,
    )
```

profile of v0, /device:TPU:0, one launch (start us, length us, event | category | flops | bytes accessed | tf_op | source)
XLA Modules:
  0.0 58.4 jit_solution(8170822670932246219)
XLA Ops:
  0.0 1.6 %fusion.66 = (f32[1]{0:T(128)}, f32[1]{0:T(128)}, f32[1]{0:T(128)}, f32[1]{0:T(128)}, f32[1]{0:T(128)}, /*index=5*/f32[1]{0:T(128)}, f32[1]{0:T(128)}, f32[1]{0:T(128)}) fusion(f32[8]{0:T(128)} %param.6), kind=kLoop, calls=%fused_computation.212 | loop fusion | bytes 64 | tf_op jit(solution)/shard_map/slice | solution.py:60
  1.6 5.9 %select_add_fusion = f32[8,16,128]{2,1,0:T(8,128)S(1)} fusion(s32[8,16,128]{2,1,0:T(8,128)} %param.8, f32[]{:T(128)} %bitcast.7, f32[]{:T(128)} %bitcast.6, f32[]{:T(128)} %bitcast.5, f32[]{:T(128)} %bitcast.4, f32[]{:T(128)} %bitcast.3, f32[]{:T(128)} %bitcast.2, f32[]{:T(128)} %bitcast.1, f32[]{:T(128)} %bitcast), kind=kLoop, calls=%fused_computation.161 | loop fusion | flops 376832 | bytes 131104 | tf_op jit(solution)/shard_map/add | solution.py:59
  7.5 1.1 %multiply_multiply_fusion = f32[3,8,16,128]{3,2,1,0:T(8,128)S(1)} fusion(f32[3,8,16,128]{3,2,1,0:T(8,128)} %param.7, s32[3,8,16,128]{3,2,1,0:T(8,128)} %param.9, f32[8,16,128]{2,1,0:T(8,128)S(1)} %select_add_fusion), kind=kLoop, calls=%fused_computation.154 | loop fusion | flops 196608 | bytes 655360 | tf_op jit(solution)/shard_map/mul | solution.py:113
  8.6 1.0 %fusion.42 = (f32[6,4,16,128]{3,2,1,0:T(8,128)S(1)}, f32[6,4,16,128]{3,2,1,0:T(8,128)S(1)}) fusion(f32[3,8,16,128]{3,2,1,0:T(8,128)} %param.5, f32[3,8,16,128]{3,2,1,0:T(8,128)S(1)} %multiply_multiply_fusion), kind=kLoop, calls=%fused_computation.142 | loop fusion | flops 98304 | bytes 786432 | tf_op jit(solution)/shard_map/concatenate | solution.py:113
  9.6 3.0 %collective-permute-start = (f32[6,4,16,128]{3,2,1,0:T(8,128)S(1)}, f32[6,4,16,128]{3,2,1,0:T(8,128)S(1)}, u32[]{:S(2)}, u32[]{:S(2)}) collective-permute-start(f32[6,4,16,128]{3,2,1,0:T(8,128)S(1)} %get-tuple-element.101), channel_id=1, source_target_pairs={{0,8},{8,16},{16,24},{24,0},{1,9},{9,17},{17,25},{25,1},{2,10},{10... | collective-permute-start | bytes 589832 | tf_op jit(solution)/shard_map/ppermute | solution.py:17
  12.6 1.0 %collective-permute-start.1 = (f32[6,4,16,128]{3,2,1,0:T(8,128)S(1)}, f32[6,4,16,128]{3,2,1,0:T(8,128)S(1)}, u32[]{:S(2)}, u32[]{:S(2)}) collective-permute-start(f32[6,4,16,128]{3,2,1,0:T(8,128)S(1)} %get-tuple-element.102), channel_id=1, source_target_pairs={{8,0},{16,8},{24,16},{0,24},{9,1},{17,9},{25,17},{1,25},{10,2},{18... | collective-permute-start | bytes 589832 | tf_op jit(solution)/shard_map/ppermute | solution.py:19
  13.6 5.7 %collective-permute-done = f32[6,4,16,128]{3,2,1,0:T(8,128)S(1)} collective-permute-done((f32[6,4,16,128]{3,2,1,0:T(8,128)S(1)}, f32[6,4,16,128]{3,2,1,0:T(8,128)S(1)}, u32[]{:S(2)}, u32[]{:S(2)}) %collective-permute-start) | collective-permute-done | bytes 196640 | tf_op jit(solution)/shard_map/ppermute | solution.py:17
  19.3 3.6 %collective-permute-done.1 = f32[6,4,16,128]{3,2,1,0:T(8,128)S(1)} collective-permute-done((f32[6,4,16,128]{3,2,1,0:T(8,128)S(1)}, f32[6,4,16,128]{3,2,1,0:T(8,128)S(1)}, u32[]{:S(2)}, u32[]{:S(2)}) %collective-permute-start.1) | collective-permute-done | bytes 196640 | tf_op jit(solution)/shard_map/ppermute | solution.py:19
  22.9 0.1 pad_maximum_fusion.15
  23.0 0.1 collective-permute-start.2
  23.1 0.5 collective-permute-start.3
  23.6 0.9 %collective-permute-done.2 = f32[6,16,4,128]{3,2,1,0:T(4,128)S(1)} collective-permute-done((f32[6,16,4,128]{3,2,1,0:T(4,128)S(1)}, f32[6,16,4,128]{3,2,1,0:T(4,128)S(1)}, u32[]{:S(2)}, u32[]{:S(2)}) %collective-permute-start.2) | collective-permute-done | bytes 196640 | tf_op jit(solution)/shard_map/ppermute | solution.py:17
  24.5 0.3 collective-permute-done.3
  24.8 0.2 pad_maximum_fusion.1
  25.0 0.4 fusion.63
  25.4 1.4 %copy.96 = f32[6,16,24,4]{2,1,3,0:T(8,128)} copy(f32[6,16,24,4]{3,2,1,0:T(8,128)S(1)} %get-tuple-element.65) | data formatting | bytes 73728 | tf_op jit(solution)/shard_map/slice | solution.py:14
  26.7 1.6 %collective-permute-start.4 = (f32[6,16,24,4]{2,1,3,0:T(8,128)}, f32[6,16,24,4]{2,1,3,0:T(8,128)S(1)}, u32[]{:S(2)}, u32[]{:S(2)}) collective-permute-start(f32[6,16,24,4]{2,1,3,0:T(8,128)} %copy.96), channel_id=1, source_target_pairs={{0,1},{1,2},{2,3},{3,0},{4,5},{5,6},{6,7},{7,4},{8,9},{9,10},{10,1... | collective-permute-start | bytes 110600 | tf_op jit(solution)/shard_map/ppermute | solution.py:17
  28.3 0.7 %copy.97 = f32[6,16,24,4]{2,1,3,0:T(8,128)S(1)} copy(f32[6,16,24,4]{3,2,1,0:T(8,128)S(1)} %get-tuple-element.66) | data formatting | bytes 73728 | tf_op jit(solution)/shard_map/slice | solution.py:13
  29.0 2.3 %collective-permute-start.5 = (f32[6,16,24,4]{2,1,3,0:T(8,128)S(1)}, f32[6,16,24,4]{2,1,3,0:T(8,128)}, u32[]{:S(2)}, u32[]{:S(2)}) collective-permute-start(f32[6,16,24,4]{2,1,3,0:T(8,128)S(1)} %copy.97), channel_id=1, source_target_pairs={{1,0},{2,1},{3,2},{0,3},{5,4},{6,5},{7,6},{4,7},{9,8},{10,9},{11,1... | collective-permute-start | bytes 110600 | tf_op jit(solution)/shard_map/ppermute | solution.py:19
  31.3 5.3 %collective-permute-done.4 = f32[6,16,24,4]{2,1,3,0:T(8,128)S(1)} collective-permute-done((f32[6,16,24,4]{2,1,3,0:T(8,128)}, f32[6,16,24,4]{2,1,3,0:T(8,128)S(1)}, u32[]{:S(2)}, u32[]{:S(2)}) %collective-permute-start.4) | collective-permute-done | bytes 36896 | tf_op jit(solution)/shard_map/ppermute | solution.py:17
  36.6 0.6 %copy.98 = f32[6,16,24,4]{3,2,1,0:T(8,128)S(1)} copy(f32[6,16,24,4]{2,1,3,0:T(8,128)S(1)} %collective-permute-done.4) | data formatting | bytes 73728 | tf_op jit(solution)/shard_map/ppermute | solution.py:17
  37.2 2.9 %collective-permute-done.5 = f32[6,16,24,4]{2,1,3,0:T(8,128)} collective-permute-done((f32[6,16,24,4]{2,1,3,0:T(8,128)S(1)}, f32[6,16,24,4]{2,1,3,0:T(8,128)}, u32[]{:S(2)}, u32[]{:S(2)}) %collective-permute-start.5) | collective-permute-done | bytes 36896 | tf_op jit(solution)/shard_map/ppermute | solution.py:19
  40.1 1.6 %copy.99 = f32[6,16,24,4]{3,2,1,0:T(8,128)S(1)} copy(f32[6,16,24,4]{2,1,3,0:T(8,128)} %collective-permute-done.5) | data formatting | bytes 73728 | tf_op jit(solution)/shard_map/ppermute | solution.py:19
  41.7 1.4 %pad_maximum_fusion = f32[6,16,24,136]{3,2,1,0:T(8,128)S(1)} fusion(f32[6,16,24,4]{3,2,1,0:T(8,128)S(1)} %copy.99, f32[6,16,4,128]{3,2,1,0:T(4,128)S(1)} %collective-permute-done.3, f32[6,4,16,128]{3,2,1,0:T(8,128)S(1)} %collective-permute-done.1, f32[3,8,16,128]{3,2,1,0:T(8,128)S(1)} %multiply_multiply_fusion, f32[3,8,16,128]{3,2,1,0:T(8,128)S(1)} %copy-done, ...), kind=kLoop, calls=%fused_computation | loop fusion | flops 2193408 | bytes 2506752 | tf_op jit(solution)/shard_map/concatenate | solution.py:15
  43.1 0.2 fusion.49
  43.3 0.6 broadcast_select_fusion
  43.9 0.1 slice_bitcast_fusion.6
  44.0 0.1 slice_bitcast_fusion.57
  44.1 0.3 slice_bitcast_fusion.67
  44.4 0.1 slice_bitcast_fusion.68
  44.5 0.1 fusion.61
  44.6 0.4 fusion.24
  45.1 0.1 slice_bitcast_fusion.29
  45.2 0.1 slice_bitcast_fusion.30
  45.5 0.3 fusion.19
  45.9 0.3 fusion.23
  46.2 0.1 fusion.26
  46.3 2.7 %slice_multiply_fusion.6 = (f32[3,14,22,134]{3,2,1,0:T(8,128)S(1)}, f32[3,14,22,134]{3,2,1,0:T(8,128)S(1)}, f32[3,14,22,134]{3,2,1,0:T(8,128)S(1)}, f32[3,14,22,134]{3,2,1,0:T(8,128)S(1)}) fusion(f32[3,16,24,136]{3,2,1,0:T(8,128)S(1)} %get-tuple-element.12, f32[3,16,24,136]{3,2,1,0:T(8,128)S(1)} %get-tuple-element.119, ...), kind=kLoop, calls=%fused_computation.197 | loop fusion | flops 1485792 | bytes 6693672 | tf_op jit(solution)/shard_map/mul | solution.py:99
  49.1 0.1 slice_bitcast_fusion.15
  49.2 0.2 slice_bitcast_fusion.61
  49.5 0.2 slice_bitcast_fusion.64
  49.7 0.1 fusion.64
  49.8 0.4 fusion.33
  50.2 0.1 slice_bitcast_fusion.31
  50.3 0.1 slice_bitcast_fusion.32
  50.6 0.3 fusion.28
  51.0 0.3 fusion.32
  51.2 0.1 fusion.35
  51.4 1.7 %fusion.14 = f32[3,12,20,132]{3,2,1,0:T(8,128)S(1)} fusion(f32[3,14,22,134]{3,2,1,0:T(8,128)S(1)} %get-tuple-element.11, f32[1,14,22,134]{3,2,1,0:T(8,128)S(1)} %fusion.35, f32[3,14,22,134]{3,2,1,0:T(8,128)S(1)} %get-tuple-element.10, f32[3,14,22,134]{3,2,1,0:T(8,128)S(1)} %get-tuple-element.22, f32[1,14,22,134]{3,2,1,0:T(8,128)S(1)} %get-tuple-element.8, ...), kind=kLoop, calls=%fused_computation.28 | loop fusion | flops 950400 | bytes 3156384 | tf_op jit(solution)/shard_map/mul | solution.py:127
  53.2 0.1 slice_bitcast_fusion.35
  53.4 0.2 subtract_add_fusion
  53.6 0.1 fusion.17
  53.7 0.1 fusion.57
  53.8 0.4 fusion.55
  54.2 0.2 fusion.60
  54.4 0.4 fusion.56
  54.8 0.2 fusion.58
  55.0 1.1 %fusion.5 = f32[4,12,20,132]{3,2,1,0:T(8,128)S(1)} fusion(f32[4,1,20,132]{3,2,1,0:T(8,128)S(1)} %get-tuple-element.47, f32[4,11,20,132]{3,2,1,0:T(8,128)S(1)} %get-tuple-element.49, f32[4,11,20,132]{3,2,1,0:T(8,128)S(1)} %get-tuple-element.48, f32[4,1,20,132]{3,2,1,0:T(8,128)S(1)} %get-tuple-element.46, f32[4,12,1,132]{3,2,1,0:T(1,128)S(1)} %get-tuple-element.43, ...), kind=kLoop, calls=%fused_computation.10 | loop fusion | flops 2534400 | bytes 4055040 | tf_op jit(solution)/shard_map/add | solution.py:88
  56.1 0.1 slice_bitcast_fusion.25
  56.3 0.1 slice_bitcast_fusion.18
  56.4 0.1 slice_bitcast_fusion.19
  56.6 0.3 fusion.37
  56.9 0.6 %copy-done.1 = s32[3,8,16,128]{3,2,1,0:T(8,128)S(1)} copy-done((s32[3,8,16,128]{3,2,1,0:T(8,128)S(1)}, s32[3,8,16,128]{3,2,1,0:T(8,128)}, u32[]{:S(2)}) %copy-start.1) | copy-done | bytes 196632
  57.6 0.9 %fusion.44 = f32[3,8,16,128]{3,2,1,0:T(8,128)} fusion(f32[1,12,20,132]{3,2,1,0:T(8,128)S(1)} %get-tuple-element.30, f32[1,12,20,132]{3,2,1,0:T(8,128)S(1)} %get-tuple-element.29, f32[1,12,20,132]{3,2,1,0:T(8,128)S(1)} %get-tuple-element.28, f32[3,14,22,134]{3,2,1,0:T(8,128)S(1)} %get-tuple-element.11, s32[3,8,16,128]{3,2,1,0:T(8,128)S(1)} %copy-done.1), kind=kLoop, calls=%fused_computation.145 | loop fusion | flops 294912 | bytes 969984 | tf_op jit(solution)/shard_map/add | solution.py:128
  (47 shorter events, 0.9 us)
Async XLA Ops:
  0.0 22.9 %copy-start = (f32[3,8,16,128]{3,2,1,0:T(8,128)S(1)}, f32[3,8,16,128]{3,2,1,0:T(8,128)}, u32[]{:S(2)}) copy-start(f32[3,8,16,128]{3,2,1,0:T(8,128)} %param.5) | copy-start | bytes 589828
  9.6 9.7 %collective-permute-start = (f32[6,4,16,128]{3,2,1,0:T(8,128)S(1)}, f32[6,4,16,128]{3,2,1,0:T(8,128)S(1)}, u32[]{:S(2)}, u32[]{:S(2)}) collective-permute-start(f32[6,4,16,128]{3,2,1,0:T(8,128)S(1)} %get-tuple-element.101), channel_id=1, source_target_pairs={{0,8},{8,16},{16,24},{24,0},{1,9},{9,17},{17,25},{25,1},{2,10},{10... | collective-permute-start | bytes 589832 | tf_op jit(solution)/shard_map/ppermute | solution.py:17
  12.6 10.3 %collective-permute-start.1 = (f32[6,4,16,128]{3,2,1,0:T(8,128)S(1)}, f32[6,4,16,128]{3,2,1,0:T(8,128)S(1)}, u32[]{:S(2)}, u32[]{:S(2)}) collective-permute-start(f32[6,4,16,128]{3,2,1,0:T(8,128)S(1)} %get-tuple-element.102), channel_id=1, source_target_pairs={{8,0},{16,8},{24,16},{0,24},{9,1},{17,9},{25,17},{1,25},{10,2},{18... | collective-permute-start | bytes 589832 | tf_op jit(solution)/shard_map/ppermute | solution.py:19
  23.0 1.5 %collective-permute-start.2 = (f32[6,16,4,128]{3,2,1,0:T(4,128)S(1)}, f32[6,16,4,128]{3,2,1,0:T(4,128)S(1)}, u32[]{:S(2)}, u32[]{:S(2)}) collective-permute-start(f32[6,16,4,128]{3,2,1,0:T(4,128)S(1)} %get-tuple-element.83), channel_id=1, source_target_pairs={{0,4},{4,0},{1,5},{5,1},{2,6},{6,2},{3,7},{7,3},{8,12},{12,8},{9,1... | collective-permute-start | bytes 589832 | tf_op jit(solution)/shard_map/ppermute | solution.py:17
  23.1 1.7 %collective-permute-start.3 = (f32[6,16,4,128]{3,2,1,0:T(4,128)S(1)}, f32[6,16,4,128]{3,2,1,0:T(4,128)S(1)}, u32[]{:S(2)}, u32[]{:S(2)}) collective-permute-start(f32[6,16,4,128]{3,2,1,0:T(4,128)S(1)} %get-tuple-element.84), channel_id=1, source_target_pairs={{4,0},{0,4},{5,1},{1,5},{6,2},{2,6},{7,3},{3,7},{12,8},{8,12},{13,... | collective-permute-start | bytes 589832 | tf_op jit(solution)/shard_map/ppermute | solution.py:19
  26.7 9.9 %collective-permute-start.4 = (f32[6,16,24,4]{2,1,3,0:T(8,128)}, f32[6,16,24,4]{2,1,3,0:T(8,128)S(1)}, u32[]{:S(2)}, u32[]{:S(2)}) collective-permute-start(f32[6,16,24,4]{2,1,3,0:T(8,128)} %copy.96), channel_id=1, source_target_pairs={{0,1},{1,2},{2,3},{3,0},{4,5},{5,6},{6,7},{7,4},{8,9},{9,10},{10,1... | collective-permute-start | bytes 110600 | tf_op jit(solution)/shard_map/ppermute | solution.py:17
  29.0 11.1 %collective-permute-start.5 = (f32[6,16,24,4]{2,1,3,0:T(8,128)S(1)}, f32[6,16,24,4]{2,1,3,0:T(8,128)}, u32[]{:S(2)}, u32[]{:S(2)}) collective-permute-start(f32[6,16,24,4]{2,1,3,0:T(8,128)S(1)} %copy.97), channel_id=1, source_target_pairs={{1,0},{2,1},{3,2},{0,3},{5,4},{6,5},{7,6},{4,7},{9,8},{10,9},{11,1... | collective-permute-start | bytes 110600 | tf_op jit(solution)/shard_map/ppermute | solution.py:19
  56.6 0.9 %copy-start.1 = (s32[3,8,16,128]{3,2,1,0:T(8,128)S(1)}, s32[3,8,16,128]{3,2,1,0:T(8,128)}, u32[]{:S(2)}) copy-start(s32[3,8,16,128]{3,2,1,0:T(8,128)} %param.9) | copy-start | bytes 589828
where the time goes:
time: 58.8 us; the launch traced here: 58.4 us
  other arithmetic  19.7 us (34%)
  waiting for transfers between devices  18.7 us (32%)
  local copies, waits for them, and re-layouts  10.9 us (19%)
  starting transfers between devices  8.48 us (14%)
  between operations  0.63 us (1%)
    ppermute x3, waiting for transfers between devices, with_halo(): lax.ppermute(tail, axis, [(i, (i + 1) % count) for i in range(count)])  11.9 us
    ppermute x3, waiting for transfers between devices, with_halo(): lax.ppermute(head, axis, [((i + 1) % count, i) for i in range(count)])  6.76 us
    add x1, other arithmetic, conductance(): total + jnp.where(region == number, conductivity[number], jnp.zeros((), c...  5.92 us
    ppermute x3, starting transfers between devices, with_halo(): lax.ppermute(tail, axis, [(i, (i + 1) % count) for i in range(count)])  4.67 us
    ppermute x3, starting transfers between devices, with_halo(): lax.ppermute(head, axis, [((i + 1) % count, i) for i in range(count)])  3.81 us
    mul x2, other arithmetic, operator_shrunk(): masked = keeping * field  3.3 us
    slice x2, local copies, waits for them, and re-layouts, with_halo(): lax.slice_in_dim(cells, cells.shape[dim] - width, cells.shape[dim], axis=...  1.75 us
    mul x1, other arithmetic, on_device(): correction = keeping * crop(nodal_part(inner_keep * residual_wide), 2)  1.73 us
  transfers between devices with their start and end apart: 6, of which 6 were waited for; matrix products, arithmetic and copies ran while one was open for 2% of the time, Pallas kernels for 0%

commit v1 on v0

v1 whole, which is shorter than its diff:
```python
import functools

import jax
import jax.numpy as jnp
from jax import lax
from jax.experimental import pallas as pl
from jax.experimental.pallas import tpu as pltpu
from jax.sharding import PartitionSpec as P

damping = 0.8
c_node = 0.8 / 7.0
MESH = pl.DeviceIdType.MESH
PAD = 4
SEG = 16


def rot(v, shift, axis):
    return pltpu.roll(v, shift % v.shape[axis], axis)


def y_up(v):
    return rot(v, -1, 0)


def y_down(v):
    return rot(v, 1, 0)


def z_up(v):
    return rot(v, -1, 1)


def z_down(v):
    return rot(v, 1, 1)


def face_zero(u1, u2):
    return (y_up(u2) - u2) - (z_up(u1) - u1)


def face_one(u0, u2, u2p):
    return (z_up(u0) - u0) - (u2p - u2)


def face_two(u0, u1, u1p):
    return (u1p - u1) - (y_up(u0) - u0)


def edges(f0, f1, f2, f1m, f2m):
    return (
        (z_down(f1) - f1) - (y_down(f2) - f2),
        (f2m - f2) - (z_down(f0) - f0),
        (y_down(f0) - f0) - (f1m - f1),
    )


def jacobi_scale(ks):
    return damping / jnp.where(ks > 0.0, 4.0 + ks, 1.0)


def start_iter(rhs, ks):
    return jnp.where(ks > 0.0, jacobi_scale(ks) * rhs, 0.0)


def next_iter(rhs, ks, u, cc):
    new = u + jacobi_scale(ks) * (rhs - (cc + ks * u))
    return jnp.where(ks > 0.0, new, 0.0)


def masked_residual(rhs, ks, u, cc):
    return jnp.where(ks > 0.0, rhs - (cc + ks * u), 0.0)


def nodal_rhs(m0, m0m, m1, m2):
    m1m, m2m = y_down(m1), z_down(m2)
    return (
        (m0m - m0) + (m1m - m1) + (m2m - m2),
        (m0 + m0m) * 0.5,
        (m1 + m1m) * 0.5,
        (m2 + m2m) * 0.5,
    )


def nodal_step(r, rm, rp):
    around = (rm + rp) + (y_up(r) + y_down(r)) + (z_up(r) + z_down(r))
    return (1.2 * c_node) * r + (c_node * c_node) * around


def finish(rhs, ks, u, corr):
    fixed = damping * rhs
    fixed = fixed + damping * (rhs - fixed)
    return jnp.where(ks > 0.0, u + corr, fixed)


def kernel(
    sizes, nx, ny, nz, cond, rhs_ref, frac_ref, reg_ref, flag_ref, out_ref,
    e, w, wz, xs, xr, ys, yr, u1, u2, mm, rr, send, recv,
):
    gx, gy, gz = sizes
    ix, iy, iz = lax.axis_index("gx"), lax.axis_index("gy"), lax.axis_index("gz")
    tiles = nx * SEG // nz
    planes = nx + 2 * PAD
    per = nz // SEG

    def device(axis, step):
        pos = {"gx": ix, "gy": iy, "gz": iz}
        size = {"gx": gx, "gy": gy, "gz": gz}
        return {axis: lax.rem(pos[axis] + (step + size[axis]), size[axis])}

    partners = [device("gx", 1), device("gx", -1), device("gz", 1), device("gz", -1), device("gy", 1)]
    if gy > 2:
        partners.append(device("gy", -1))
    barrier = pltpu.get_barrier_semaphore()
    for partner in partners:
        pl.semaphore_signal(barrier, inc=1, device_id=partner, device_id_type=MESH)

    lane = lax.broadcasted_iota(jnp.int32, (ny, nz), 1)
    slot = lane // SEG

    packs = [[None] * tiles for _ in range(6)]
    for x in range(nx):
        region = reg_ref[x]
        sigma = jnp.zeros((ny, nz), jnp.float32)
        for number in range(cond.shape[0]):
            sigma = jnp.where(region == number, cond[number], sigma)
        for k in range(3):
            ks = jnp.where(flag_ref[k, x] == 0, sigma * frac_ref[k, x], 0.0)
            for f, v in ((k, rhs_ref[k, x]), (3 + k, ks)):
                e[f, PAD + x, 0:ny, :] = v
                t, j = divmod(x, per)
                piece = rot(v, 8 + SEG * j, 1)
                old = packs[f][t]
                packs[f][t] = piece if old is None else jnp.where(slot == j, piece, old)
    for f in range(6):
        for t in range(tiles):
            w[f, t] = packs[f][t]

    pl.semaphore_wait(barrier, len(partners))

    def copy(number, src, dst, where):
        made = pltpu.make_async_remote_copy(
            src_ref=src, dst_ref=dst, send_sem=send.at[number], recv_sem=recv.at[number],
            device_id=where, device_id_type=MESH,
        )
        made.start()
        return made

    z_copies = [
        copy(0, w, wz.at[0], device("gz", 1)),
        copy(1, w, wz.at[1], device("gz", -1)),
    ]
    x_copies = [
        copy(2, e.at[:, pl.ds(PAD + nx - 3, 3), pl.ds(0, ny)], e.at[:, pl.ds(1, 3), pl.ds(0, ny)], device("gx", 1)),
        copy(3, e.at[:, pl.ds(PAD, 4), pl.ds(0, ny)], e.at[:, pl.ds(PAD + nx, 4), pl.ds(0, ny)], device("gx", -1)),
    ]
    for c in z_copies:
        c.wait()
    left = (lane % SEG) < 8
    base_a = planes
    base_b = planes + tiles + 1
    half = nz // 2
    for f in range(6):
        ab = []
        for t in range(tiles):
            own = w[f, t]
            a = jnp.where(left, own, wz[1, f, t])
            b = jnp.where(left, wz[0, f, t], own)
            e[f, base_a + t, 0:ny, :] = a
            e[f, base_b + t, 0:ny, :] = b
            ab.append((a, b))
        xs[0, f] = jnp.where(lane < half, rot(ab[-1][1], half, 1), ab[-1][0])
        xs[1, f] = jnp.where(lane < half, ab[0][0], rot(ab[0][1], half, 1))
    x_copies += [
        copy(4, xs.at[0], xr.at[0], device("gx", 1)),
        copy(5, xs.at[1], xr.at[1], device("gx", -1)),
    ]
    for c in x_copies:
        c.wait()
    for f in range(6):
        minus, plus = xr[0, f], xr[1, f]
        e[f, base_a + tiles, 0:ny, :] = jnp.where(lane < half, plus, minus)
        e[f, base_b + tiles, 0:ny, :] = rot(jnp.where(lane < half, minus, plus), half, 1)

    total = planes + 2 * (tiles + 1)
    row = lax.broadcasted_iota(jnp.int32, (8, nz), 0)
    for f in range(6):
        for p in range(1, total):
            ys[f, p] = jnp.where(row < 4, e[f, p, 0:8, :], e[f, p, ny - 8:ny, :])
    if gy == 2:
        copy(6, ys, yr.at[0], device("gy", 1)).wait()
    else:
        c0 = copy(6, ys, yr.at[0], device("gy", -1))
        c1 = copy(7, ys, yr.at[1], device("gy", 1))
        c0.wait()
        c1.wait()
    for f in range(6):
        for p in range(1, total):
            tile = yr[0, f, p] if gy == 2 else jnp.where(row < 4, yr[0, f, p], yr[1, f, p])
            e[f, p, ny:ny + 8, :] = tile

    lane24 = lax.broadcasted_iota(jnp.int32, (ny + 8, nz), 1)

    def x_up(vs):
        rs = [rot(v, -SEG, 1) for v in vs]
        return [jnp.where(lane24 < nz - SEG, rs[t], rs[(t + 1) % len(rs)]) for t in range(len(rs))]

    def x_down(vs):
        rs = [rot(v, SEG, 1) for v in vs]
        return [jnp.where(lane24 >= SEG, rs[t], rs[t - 1]) for t in range(len(rs))]

    count = tiles + 1

    def strip_curl(u):
        u1p, u2p = x_up(u[1]), x_up(u[2])
        f0 = [face_zero(u[1][t], u[2][t]) for t in range(count)]
        f1 = [face_one(u[0][t], u[2][t], u2p[t]) for t in range(count)]
        f2 = [face_two(u[0][t], u[1][t], u1p[t]) for t in range(count)]
        f1m, f2m = x_down(f1), x_down(f2)
        out = [edges(f0[t], f1[t], f2[t], f1m[t], f2m[t]) for t in range(count)]
        return [[out[t][k] for t in range(count)] for k in range(3)]

    ends = []
    for base in (base_a, base_b):
        def sr(k, t):
            return e[k, base + t]

        def sk(k, t):
            return e[3 + k, base + t]

        span = range(count)
        u = [[start_iter(sr(k, t), sk(k, t)) for t in span] for k in range(3)]
        cc = strip_curl(u)
        u = [[next_iter(sr(k, t), sk(k, t), u[k][t], cc[k][t]) for t in span] for k in range(3)]
        cc = strip_curl(u)
        m = [[masked_residual(sr(k, t), sk(k, t), u[k][t], cc[k][t]) for t in span] for k in range(3)]
        m0m = x_down(m[0])
        r = [nodal_rhs(m[0][t], m0m[t], m[1][t], m[2][t]) for t in span]
        s = []
        for q in range(4):
            rq = [r[t][q] for t in span]
            rm, rp = x_down(rq), x_up(rq)
            s.append([nodal_step(rq[t], rm[t], rp[t]) for t in span])
        s0p, s1p = x_up(s[0]), x_up(s[1])
        result = []
        for t in range(tiles):
            corr = (
                (s0p[t] - s[0][t]) + (s[1][t] + s1p[t]) * 0.5,
                (y_up(s[0][t]) - s[0][t]) + (s[2][t] + y_up(s[2][t])) * 0.5,
                (z_up(s[0][t]) - s[0][t]) + (s[3][t] + z_up(s[3][t])) * 0.5,
            )
            result.append([finish(sr(k, t), sk(k, t), u[k][t], corr[k])[0:ny] for k in range(3)])
        ends.append(result)
    for t in range(tiles):
        for k in range(3):
            w[k, t] = jnp.where(left, ends[0][t][k], ends[1][t][k])

    for p in range(1, planes):
        for k in range(3):
            u1[k, p] = start_iter(e[k, p], e[3 + k, p])

    def curl_sweep(u, lo, hi, emit):
        def faces(p):
            v0, v1, v2 = u[0, p], u[1, p], u[2, p]
            return face_one(v0, v2, u[2, p + 1]), face_two(v0, v1, u[1, p + 1])

        f1m, f2m = faces(lo - 1)
        for p in range(lo, hi):
            f1, f2 = faces(p)
            f0 = face_zero(u[1, p], u[2, p])
            cc = edges(f0, f1, f2, f1m, f2m)
            for k in range(3):
                emit(k, p, cc[k])
            f1m, f2m = f1, f2

    def emit_second(k, p, cc):
        u2[k, p] = next_iter(e[k, p], e[3 + k, p], u1[k, p], cc)

    curl_sweep(u1, PAD - 2, PAD + nx + 3, emit_second)

    def emit_masked(k, p, cc):
        mm[k, p] = masked_residual(e[k, p], e[3 + k, p], u2[k, p], cc)

    curl_sweep(u2, PAD - 1, PAD + nx + 2, emit_masked)
    p = PAD - 2
    v0, v1, v2 = u2[0, p], u2[1, p], u2[2, p]
    f1 = face_one(v0, v2, u2[2, p + 1])
    f2 = face_two(v0, v1, u2[1, p + 1])
    emit_masked(0, p, (z_down(f1) - f1) - (y_down(f2) - f2))

    p = PAD + nx + 2
    for p in range(PAD - 1, PAD + nx + 2):
        r = nodal_rhs(mm[0, p], mm[0, p - 1], mm[1, p], mm[2, p])
        for q in range(4):
            rr[q, p] = r[q]

    inner = (lane >= 4) & (lane < nz - 4)
    s_next = [nodal_step(rr[q, PAD], rr[q, PAD - 1], rr[q, PAD + 1]) for q in range(4)]
    for x in range(nx):
        p = PAD + x
        s = s_next
        s_next = [nodal_step(rr[q, p + 1], rr[q, p], rr[q, p + 2]) for q in range(4)] if x < nx - 1 else [
            nodal_step(rr[q, p + 1], rr[q, p], rr[q, p + 2]) for q in range(2)
        ]
        corr = (
            (s_next[0] - s[0]) + (s[1] + s_next[1]) * 0.5,
            (y_up(s[0]) - s[0]) + (s[2] + y_up(s[2])) * 0.5,
            (z_up(s[0]) - s[0]) + (s[3] + z_up(s[3])) * 0.5,
        )
        t, j = divmod(x, per)
        for k in range(3):
            body = finish(e[k, p, 0:ny], e[3 + k, p, 0:ny], u2[k, p, 0:ny], corr[k][0:ny])
            out_ref[k, x] = jnp.where(inner, body, rot(w[k, t], nz - 8 - SEG * j, 1))


def on_device(sizes, rhs, conductivity, fraction, region, flags):
    _, nx, ny, nz = rhs.shape
    tiles = nx * SEG // nz
    planes = nx + 2 * PAD
    total = planes + 2 * (tiles + 1)
    rows = ny + 8
    f32 = jnp.float32
    vmem = pl.BlockSpec(memory_space=pltpu.VMEM)
    sides = 1 if sizes[1] == 2 else 2
    return pl.pallas_call(
        functools.partial(kernel, sizes, nx, ny, nz),
        out_shape=jax.ShapeDtypeStruct(rhs.shape, rhs.dtype),
        in_specs=[pl.BlockSpec(memory_space=pltpu.SMEM)] + [vmem] * 4,
        out_specs=vmem,
        scratch_shapes=[
            pltpu.VMEM((6, total, rows, nz), f32),
            pltpu.VMEM((6, tiles, ny, nz), f32),
            pltpu.VMEM((2, 6, tiles, ny, nz), f32),
            pltpu.VMEM((2, 6, ny, nz), f32),
            pltpu.VMEM((2, 6, ny, nz), f32),
            pltpu.VMEM((6, total, 8, nz), f32),
            pltpu.VMEM((sides, 6, total, 8, nz), f32),
            pltpu.VMEM((3, planes, rows, nz), f32),
            pltpu.VMEM((3, planes, rows, nz), f32),
            pltpu.VMEM((3, planes, rows, nz), f32),
            pltpu.VMEM((4, planes, rows, nz), f32),
            pltpu.SemaphoreType.DMA((8,)),
            pltpu.SemaphoreType.DMA((8,)),
        ],
        compiler_params=pltpu.CompilerParams(
            collective_id=0, has_side_effects=True, vmem_limit_bytes=60 * 1024 * 1024
        ),
    )(conductivity, rhs, fraction, region, flags)


def solution(mesh):
    sizes = tuple(mesh.shape[name] for name in ("gx", "gy", "gz"))
    return jax.shard_map(
        functools.partial(on_device, sizes),
        mesh=mesh,
        in_specs=(
            P(None, "gx", "gy", "gz"),
            P(),
            P(None, "gx", "gy", "gz"),
            P("gx", "gy", "gz"),
            P(None, "gx", "gy", "gz"),
        ),
        out_specs=P(None, "gx", "gy", "gz"),
        check_vma=False,
    )
```

time: 58.8 us -> 25.3 us (0.43)
  Pallas kernels: 0 us -> 23.6 us
  other arithmetic: 19.7 us -> 0 us
  waiting for transfers between devices: 18.7 us -> 0 us
  local copies, waits for them, and re-layouts: 10.9 us -> 1.62 us
  starting transfers between devices: 8.48 us -> 0 us
  between operations: 0.63 us -> 0.01 us
    pallas_call x0 -> x1, Pallas kernels: none -> 23.6 us  [on_device(): pl.pallas_call(functools.partial(kernel, sizes, nx, ny, nz), out_shape=ja...]
    ppermute x6 -> x0, waiting for transfers between devices: 18.7 us -> none  [the longest x3 11.9 us: with_halo(): lax.ppermute(tail, axis, [(i, (i + 1) % count) for i in range(count)])]
    ppermute x6 -> x0, starting transfers between devices: 8.48 us -> none  [the longest x3 4.67 us: with_halo(): lax.ppermute(tail, axis, [(i, (i + 1) % count) for i in range(count)])]
    add x5 -> x0, other arithmetic: 8.38 us -> none  [the longest x1 5.92 us: conductance(): total + jnp.where(region == number, conductivity[number], jnp.zeros((), c...]
    mul x4 -> x0, other arithmetic: 6.09 us -> none  [the longest x2 3.3 us: operator_shrunk(): masked = keeping * field]
    slice x18 -> x0, local copies, waits for them, and re-layouts: 5.55 us -> none  [the longest x2 1.75 us: with_halo(): lax.slice_in_dim(cells, cells.shape[dim] - width, cells.shape[dim], axis=...]
    concatenate x3 -> x0, other arithmetic: 2.59 us -> none  [the longest x2 1.61 us: with_halo(): jnp.concatenate([lax.ppermute(tail, axis, [(i, (i + 1) % count) for i in...]
    sub x8 -> x0, other arithmetic: 2.27 us -> none  [the longest x2 0.75 us: curl_curl(): face_zero = forward_diff(third, 1) - forward_diff(second, 2)]
  transfers between devices with their start and end apart: 6 -> 0, of which waited for: 6 -> 0; matrix products, arithmetic and copies ran while one was open for 2% -> 0% of each run, Pallas kernels for 0% -> 0%
where the time goes in v1:
time: 25.3 us; the launch traced here: 25.2 us
  Pallas kernels  23.6 us (93%)
  local copies, waits for them, and re-layouts  1.62 us (6%)
    pallas_call x1, Pallas kernels, on_device(): pl.pallas_call(functools.partial(kernel, sizes, nx, ny, nz), out_shape=ja...  23.6 us
    unnamed x1, local copies, waits for them, and re-layouts  1.62 us

profile of v1, /device:TPU:0, one launch (start us, length us, event | category | flops | bytes accessed | tf_op | source)
XLA Modules:
  0.0 25.2 jit_solution(1563421163398057926)
XLA Ops:
  0.0 23.6 %shard_map.55 = f32[3,8,16,128]{3,2,1,0:T(8,128)} custom-call(f32[8]{0:T(128)} %cond.1, f32[3,8,16,128]{3,2,1,0:T(8,128)} %rhs_ref.1, f32[3,8,16,128]{3,2,1,0:T(8,128)} %frac_ref.1, s32[8,16,128]{2,1,0:T(8,128)} %reg_ref.1, s32[3,8,16,128]{3,2,1,0:T(8,128)} %flag_ref.1), custom_call_target="tpu_custom_call" | custom-call | tf_op jit(solution)/shard_map/pallas_call | solution.py:324
  23.6 1.6 %copy.7 = f32[3,8,16,128]{3,2,1,0:T(8,128)} copy(f32[3,8,16,128]{3,2,1,0:T(8,128)} %shard_map.55) | data formatting | bytes 393216

commit v2 on v1

--- a/solution.py
+++ b/solution.py
@@ -93,47 +93,85 @@
 
 
 def kernel(
-    sizes, nx, ny, nz, cond, rhs_ref, frac_ref, reg_ref, flag_ref, out_ref,
-    e, w, wz, xs, xr, ys, yr, u1, u2, mm, rr, send, recv,
+    sizes, nx, ny, nz, cond, rhs_hbm, frac_hbm, reg_hbm, flag_hbm, out_ref,
+    rhs_ref, frac_ref, reg_ref, flag_ref,
+    e, w, wz, kf, ds, dr, ya, yb, yra, yrb, u1, u2, mm, rr, load, send, recv,
 ):
     gx, gy, gz = sizes
-    ix, iy, iz = lax.axis_index("gx"), lax.axis_index("gy"), lax.axis_index("gz")
+    pos = {"gx": lax.axis_index("gx"), "gy": lax.axis_index("gy"), "gz": lax.axis_index("gz")}
+    size = {"gx": gx, "gy": gy, "gz": gz}
     tiles = nx * SEG // nz
     planes = nx + 2 * PAD
     per = nz // SEG
 
-    def device(axis, step):
-        pos = {"gx": ix, "gy": iy, "gz": iz}
-        size = {"gx": gx, "gy": gy, "gz": gz}
-        return {axis: lax.rem(pos[axis] + (step + size[axis]), size[axis])}
-
-    partners = [device("gx", 1), device("gx", -1), device("gz", 1), device("gz", -1), device("gy", 1)]
+    def device(**steps):
+        return {axis: lax.rem(pos[axis] + (step + size[axis]), size[axis]) for axis, step in steps.items()}
+
+    partners = [device(gx=1), device(gx=-1), device(gz=1), device(gz=-1), device(gy=1)]
+    partners += [device(gx=i, gz=j) for i in (1, -1) for j in (1, -1)]
     if gy > 2:
-        partners.append(device("gy", -1))
+        partners.append(device(gy=-1))
     barrier = pltpu.get_barrier_semaphore()
     for partner in partners:
         pl.semaphore_signal(barrier, inc=1, device_id=partner, device_id_type=MESH)
+    loads = [
+        pltpu.make_async_copy(src, dst, load.at[i])
+        for i, (src, dst) in enumerate(
+            ((reg_hbm, reg_ref), (frac_hbm, frac_ref), (flag_hbm, flag_ref), (rhs_hbm, rhs_ref))
+        )
+    ]
+    for one in loads:
+        one.start()
+    for one in loads:
+        one.wait()
 
     lane = lax.broadcasted_iota(jnp.int32, (ny, nz), 1)
     slot = lane // SEG
+    half = nz // 2
+    low_half = lane < half
+    quad = (lane % SEG) // 4
+    left = (lane % SEG) < 8
+
+    def end_piece(v, j):
+        return rot(v, 8 + SEG * j, 1)
 
     packs = [[None] * tiles for _ in range(6)]
+    outer = {nx - 3: 0, 3: 1}
+    sent_first = {}
     for x in range(nx):
         region = reg_ref[x]
         sigma = jnp.zeros((ny, nz), jnp.float32)
         for number in range(cond.shape[0]):
             sigma = jnp.where(region == number, cond[number], sigma)
+        t, j = divmod(x, per)
         for k in range(3):
             ks = jnp.where(flag_ref[k, x] == 0, sigma * frac_ref[k, x], 0.0)
-            for f, v in ((k, rhs_ref[k, x]), (3 + k, ks)):
+            rhs = rhs_ref[k, x]
+            for f, v in ((k, rhs), (3 + k, ks)):
                 e[f, PAD + x, 0:ny, :] = v
-                t, j = divmod(x, per)
-                piece = rot(v, 8 + SEG * j, 1)
+                piece = end_piece(v, j)
                 old = packs[f][t]
                 packs[f][t] = piece if old is None else jnp.where(slot == j, piece, old)
+            if x in outer:
+                first = start_iter(rhs, ks)
+                kf[outer[x], k] = first
+                sent_first[outer[x], k] = end_piece(first, j)
     for f in range(6):
         for t in range(tiles):
             w[f, t] = packs[f][t]
+    for side in range(2):
+        mine = (lane >= half) if side == 0 else low_half
+        j = (nx - 3) % per if side == 0 else 3
+        for zside, off in ((0, 8), (1, 4)):
+            tile = None
+            for f in range(6):
+                v = packs[f][tiles - 1 if side == 0 else 0]
+                if f < 3:
+                    v = jnp.where(slot == j, sent_first[side, f], v)
+                moved = rot(v, 4 * (f % 4) - off + (half if f >= 4 else 0), 1)
+                where = (quad == f % 4) & (mine if f < 4 else ~mine)
+                tile = moved if tile is None else jnp.where(where, moved, tile)
+            ds[side, zside] = tile
 
     pl.semaphore_wait(barrier, len(partners))
 
@@ -145,60 +183,113 @@
         made.start()
         return made
 
-    z_copies = [
-        copy(0, w, wz.at[0], device("gz", 1)),
-        copy(1, w, wz.at[1], device("gz", -1)),
+    own_rows = pl.ds(0, ny)
+    z_copies = [copy(0, w, wz.at[0], device(gz=1)), copy(1, w, wz.at[1], device(gz=-1))]
+    x_copies = [
+        copy(2 + 2 * side + zside, ds.at[side, zside], dr.at[side, zside], device(gx=1 - 2 * side, gz=2 * zside - 1))
+        for side in range(2) for zside in range(2)
     ]
-    x_copies = [
-        copy(2, e.at[:, pl.ds(PAD + nx - 3, 3), pl.ds(0, ny)], e.at[:, pl.ds(1, 3), pl.ds(0, ny)], device("gx", 1)),
-        copy(3, e.at[:, pl.ds(PAD, 4), pl.ds(0, ny)], e.at[:, pl.ds(PAD + nx, 4), pl.ds(0, ny)], device("gx", -1)),
+    x_copies += [
+        copy(6, e.at[:, pl.ds(PAD + nx - 2, 2), own_rows], e.at[:, pl.ds(2, 2), own_rows], device(gx=1)),
+        copy(7, e.at[:, pl.ds(PAD, 3), own_rows], e.at[:, pl.ds(PAD + nx, 3), own_rows], device(gx=-1)),
+        copy(8, kf.at[0], e.at[pl.ds(0, 3), 1, own_rows], device(gx=1)),
+        copy(9, kf.at[1, pl.ds(1, 2)], e.at[pl.ds(1, 2), PAD + nx + 3, own_rows], device(gx=-1)),
     ]
-    for c in z_copies:
-        c.wait()
-    left = (lane % SEG) < 8
+
     base_a = planes
     base_b = planes + tiles + 1
-    half = nz // 2
+    row = lax.broadcasted_iota(jnp.int32, (8, nz), 0)
+
+    def y_start(first, which, out, into):
+        for f in range(6):
+            for i, p in enumerate(which):
+                out[f, i] = jnp.where(row < 4, e[f, p, 0:8, :], e[f, p, ny - 8:ny, :])
+        if gy == 2:
+            return [copy(first, out, into.at[0], device(gy=1))]
+        return [
+            copy(first, out, into.at[0], device(gy=-1)),
+            copy(first + 1, out, into.at[1], device(gy=1)),
+        ]
+
+    def y_finish(copies, which, into):
+        for one in copies:
+            one.wait()
+        for f in range(6):
+            for i, p in enumerate(which):
+                tile = into[0, f, i] if gy == 2 else jnp.where(row < 4, into[0, f, i], into[1, f, i])
+                e[f, p, ny:ny + 8, :] = tile
+
+    def curl_sweep(u, lo, hi, emit):
+        def faces(p):
+            v0, v1, v2 = u[0, p], u[1, p], u[2, p]
+            return face_one(v0, v2, u[2, p + 1]), face_two(v0, v1, u[1, p + 1])
+
+        f1m, f2m = faces(lo - 1)
+        for p in range(lo, hi):
+            f1, f2 = faces(p)
+            f0 = face_zero(u[1, p], u[2, p])
+            cc = edges(f0, f1, f2, f1m, f2m)
+            for k in range(3):
+                emit(k, p, cc[k])
+            f1m, f2m = f1, f2
+
+    def emit_second(k, p, cc):
+        u2[k, p] = next_iter(e[k, p], e[3 + k, p], u1[k, p], cc)
+
+    def emit_masked(k, p, cc):
+        mm[k, p] = masked_residual(e[k, p], e[3 + k, p], u2[k, p], cc)
+
+    def node_range(lo, hi):
+        for p in range(lo, hi):
+            r = nodal_rhs(mm[0, p], mm[0, p - 1], mm[1, p], mm[2, p])
+            for q in range(4):
+                rr[q, p] = r[q]
+
+    def first_range(which):
+        for p in which:
+            for k in range(3):
+                u1[k, p] = start_iter(e[k, p], e[3 + k, p])
+
+    own = list(range(PAD, PAD + nx))
+    y_own = y_start(10, own, ya, yra)
+    y_finish(y_own, own, yra)
+    first_range(own)
+    curl_sweep(u1, PAD + 1, PAD + nx - 1, emit_second)
+    curl_sweep(u2, PAD + 2, PAD + nx - 2, emit_masked)
+    node_range(PAD + 3, PAD + nx - 2)
+
+    for one in z_copies:
+        one.wait()
     for f in range(6):
-        ab = []
         for t in range(tiles):
-            own = w[f, t]
-            a = jnp.where(left, own, wz[1, f, t])
-            b = jnp.where(left, wz[0, f, t], own)
-            e[f, base_a + t, 0:ny, :] = a
-            e[f, base_b + t, 0:ny, :] = b
-            ab.append((a, b))
-        xs[0, f] = jnp.where(lane < half, rot(ab[-1][1], half, 1), ab[-1][0])
-        xs[1, f] = jnp.where(lane < half, ab[0][0], rot(ab[0][1], half, 1))
-    x_copies += [
-        copy(4, xs.at[0], xr.at[0], device("gx", 1)),
-        copy(5, xs.at[1], xr.at[1], device("gx", -1)),
-    ]
-    for c in x_copies:
-        c.wait()
+            mid = w[f, t]
+            e[f, base_a + t, 0:ny, :] = jnp.where(left, mid, wz[1, f, t])
+            e[f, base_b + t, 0:ny, :] = jnp.where(left, wz[0, f, t], mid)
+    for one in x_copies:
+        one.wait()
     for f in range(6):
-        minus, plus = xr[0, f], xr[1, f]
-        e[f, base_a + tiles, 0:ny, :] = jnp.where(lane < half, plus, minus)
-        e[f, base_b + tiles, 0:ny, :] = rot(jnp.where(lane < half, minus, plus), half, 1)
-
-    total = planes + 2 * (tiles + 1)
-    row = lax.broadcasted_iota(jnp.int32, (8, nz), 0)
-    for f in range(6):
-        for p in range(1, total):
-            ys[f, p] = jnp.where(row < 4, e[f, p, 0:8, :], e[f, p, ny - 8:ny, :])
-    if gy == 2:
-        copy(6, ys, yr.at[0], device("gy", 1)).wait()
-    else:
-        c0 = copy(6, ys, yr.at[0], device("gy", -1))
-        c1 = copy(7, ys, yr.at[1], device("gy", 1))
-        c0.wait()
-        c1.wait()
-    for f in range(6):
-        for p in range(1, total):
-            tile = yr[0, f, p] if gy == 2 else jnp.where(row < 4, yr[0, f, p], yr[1, f, p])
-            e[f, p, ny:ny + 8, :] = tile
+        ends = None
+        for i in range(8):
+            if i != 4:
+                p = PAD + nx + i if i < 4 else i - 4
+                piece = end_piece(e[f, p, 0:ny, :], i)
+                ends = piece if ends is None else jnp.where(slot == i, piece, ends)
+        corner = []
+        for zside, off in ((0, 8), (1, 4)):
+            plus, minus = dr[1, zside], dr[0, zside]
+            if f < 4:
+                corner.append(rot(jnp.where(low_half, plus, minus), off - 4 * f, 1))
+            else:
+                corner.append(rot(jnp.where(low_half, minus, plus), half + off - 4 * (f - 4), 1))
+        e[f, base_a + tiles, 0:ny, :] = jnp.where(left, ends, corner[0])
+        e[f, base_b + tiles, 0:ny, :] = jnp.where(left, corner[1], ends)
+    rest = list(range(1, PAD)) + list(range(PAD + nx, planes)) + list(range(base_a, base_b + tiles + 1))
+    y_rest = y_start(12, rest, yb, yrb)
+    y_finish(y_rest, rest, yrb)
 
     lane24 = lax.broadcasted_iota(jnp.int32, (ny + 8, nz), 1)
+
+    sent = (lane24 // SEG == 3) | (lane24 // SEG == 5)
 
     def x_up(vs):
         rs = [rot(v, -SEG, 1) for v in vs]
@@ -229,6 +320,8 @@
 
         span = range(count)
         u = [[start_iter(sr(k, t), sk(k, t)) for t in span] for k in range(3)]
+        for k in range(3):
+            u[k][tiles] = jnp.where(sent, sr(k, tiles), u[k][tiles])
         cc = strip_curl(u)
         u = [[next_iter(sr(k, t), sk(k, t), u[k][t], cc[k][t]) for t in span] for k in range(3)]
         cc = strip_curl(u)
@@ -254,44 +347,21 @@
         for k in range(3):
             w[k, t] = jnp.where(left, ends[0][t][k], ends[1][t][k])
 
-    for p in range(1, planes):
-        for k in range(3):
-            u1[k, p] = start_iter(e[k, p], e[3 + k, p])
-
-    def curl_sweep(u, lo, hi, emit):
-        def faces(p):
-            v0, v1, v2 = u[0, p], u[1, p], u[2, p]
-            return face_one(v0, v2, u[2, p + 1]), face_two(v0, v1, u[1, p + 1])
-
-        f1m, f2m = faces(lo - 1)
-        for p in range(lo, hi):
-            f1, f2 = faces(p)
-            f0 = face_zero(u[1, p], u[2, p])
-            cc = edges(f0, f1, f2, f1m, f2m)
-            for k in range(3):
-                emit(k, p, cc[k])
-            f1m, f2m = f1, f2
-
-    def emit_second(k, p, cc):
-        u2[k, p] = next_iter(e[k, p], e[3 + k, p], u1[k, p], cc)
-
-    curl_sweep(u1, PAD - 2, PAD + nx + 3, emit_second)
-
-    def emit_masked(k, p, cc):
-        mm[k, p] = masked_residual(e[k, p], e[3 + k, p], u2[k, p], cc)
-
-    curl_sweep(u2, PAD - 1, PAD + nx + 2, emit_masked)
+    for k in range(3):
+        u1[k, 1] = e[k, 1]
+        u1[k, planes - 1] = e[k, planes - 1]
+    first_range(list(range(2, PAD)) + list(range(PAD + nx, planes - 1)))
+    curl_sweep(u1, PAD - 2, PAD + 1, emit_second)
+    curl_sweep(u1, PAD + nx - 1, PAD + nx + 3, emit_second)
+    curl_sweep(u2, PAD - 1, PAD + 2, emit_masked)
+    curl_sweep(u2, PAD + nx - 2, PAD + nx + 2, emit_masked)
     p = PAD - 2
     v0, v1, v2 = u2[0, p], u2[1, p], u2[2, p]
     f1 = face_one(v0, v2, u2[2, p + 1])
     f2 = face_two(v0, v1, u2[1, p + 1])
     emit_masked(0, p, (z_down(f1) - f1) - (y_down(f2) - f2))
-
-    p = PAD + nx + 2
-    for p in range(PAD - 1, PAD + nx + 2):
-        r = nodal_rhs(mm[0, p], mm[0, p - 1], mm[1, p], mm[2, p])
-        for q in range(4):
-            rr[q, p] = r[q]
+    node_range(PAD - 1, PAD + 3)
+    node_range(PAD + nx - 2, PAD + nx + 2)
 
     inner = (lane >= 4) & (lane < nz - 4)
     s_next = [nodal_step(rr[q, PAD], rr[q, PAD - 1], rr[q, PAD + 1]) for q in range(4)]
@@ -317,32 +387,41 @@
     tiles = nx * SEG // nz
     planes = nx + 2 * PAD
     total = planes + 2 * (tiles + 1)
+    rest = 2 * PAD - 1 + 2 * (tiles + 1)
     rows = ny + 8
     f32 = jnp.float32
-    vmem = pl.BlockSpec(memory_space=pltpu.VMEM)
+    hbm = pl.BlockSpec(memory_space=pl.ANY)
     sides = 1 if sizes[1] == 2 else 2
     return pl.pallas_call(
         functools.partial(kernel, sizes, nx, ny, nz),
-        out_shape=jax.ShapeDtypeStruct(rhs.shape, rhs.dtype),
-        in_specs=[pl.BlockSpec(memory_space=pltpu.SMEM)] + [vmem] * 4,
-        out_specs=vmem,
+        out_shape=pltpu.VMEM(rhs.shape, rhs.dtype),
+        in_specs=[pl.BlockSpec(memory_space=pltpu.SMEM)] + [hbm] * 4,
+        out_specs=pl.BlockSpec(memory_space=pltpu.VMEM),
         scratch_shapes=[
+            pltpu.VMEM(rhs.shape, f32),
+            pltpu.VMEM(rhs.shape, f32),
+            pltpu.VMEM(region.shape, jnp.int32),
+            pltpu.VMEM(flags.shape, jnp.int32),
             pltpu.VMEM((6, total, rows, nz), f32),
             pltpu.VMEM((6, tiles, ny, nz), f32),
             pltpu.VMEM((2, 6, tiles, ny, nz), f32),
-            pltpu.VMEM((2, 6, ny, nz), f32),
-            pltpu.VMEM((2, 6, ny, nz), f32),
-            pltpu.VMEM((6, total, 8, nz), f32),
-            pltpu.VMEM((sides, 6, total, 8, nz), f32),
+            pltpu.VMEM((2, 3, ny, nz), f32),
+            pltpu.VMEM((2, 2, ny, nz), f32),
+            pltpu.VMEM((2, 2, ny, nz), f32),
+            pltpu.VMEM((6, nx, 8, nz), f32),
+            pltpu.VMEM((6, rest, 8, nz), f32),
+            pltpu.VMEM((sides, 6, nx, 8, nz), f32),
+            pltpu.VMEM((sides, 6, rest, 8, nz), f32),
             pltpu.VMEM((3, planes, rows, nz), f32),
             pltpu.VMEM((3, planes, rows, nz), f32),
             pltpu.VMEM((3, planes, rows, nz), f32),
             pltpu.VMEM((4, planes, rows, nz), f32),
-            pltpu.SemaphoreType.DMA((8,)),
-            pltpu.SemaphoreType.DMA((8,)),
+            pltpu.SemaphoreType.DMA((4,)),
+            pltpu.SemaphoreType.DMA((14,)),
+            pltpu.SemaphoreType.DMA((14,)),
         ],
         compiler_params=pltpu.CompilerParams(
-            collective_id=0, has_side_effects=True, vmem_limit_bytes=60 * 1024 * 1024
+            collective_id=0, has_side_effects=True, vmem_limit_bytes=40 * 1024 * 1024
         ),
     )(conductivity, rhs, fraction, region, flags)
 

time: 25.3 us -> 24.3 us (0.960)
  Pallas kernels: 23.6 us -> 19.1 us
  local copies, waits for them, and re-layouts: 1.62 us -> 4.95 us
    pallas_call x1, Pallas kernels: 23.6 us -> 19.1 us  [on_device(): pl.pallas_call(functools.partial(kernel, sizes, nx, ny, nz), out_shape=pl...]
    unnamed x1 -> x11, local copies, waits for them, and re-layouts: 1.62 us -> 4.95 us
where the time goes in v2:
time: 24.3 us; the launch traced here: 24.1 us
  Pallas kernels  19.1 us (79%)
  local copies, waits for them, and re-layouts  4.95 us (20%)
    pallas_call x1, Pallas kernels, on_device(): pl.pallas_call(functools.partial(kernel, sizes, nx, ny, nz), out_shape=pl...  19.1 us
    unnamed x11, local copies, waits for them, and re-layouts  4.95 us

profile of v2, /device:TPU:0, one launch (start us, length us, event | category | flops | bytes accessed | tf_op | source)
XLA Modules:
  0.0 24.1 jit_solution(15962914232241888552)
XLA Ops:
  0.0 0.0 copy-start
  0.0 0.9 %copy-done = f32[3,8,16,128]{3,2,1,0:T(8,128)S(1)} copy-done((f32[3,8,16,128]{3,2,1,0:T(8,128)S(1)}, f32[3,8,16,128]{3,2,1,0:T(8,128)}, u32[]{:S(2)}) %copy-start) | copy-done | bytes 196632
  0.9 0.0 copy-start.1
  0.9 0.9 %copy-done.1 = f32[3,8,16,128]{3,2,1,0:T(8,128)S(1)} copy-done((f32[3,8,16,128]{3,2,1,0:T(8,128)S(1)}, f32[3,8,16,128]{3,2,1,0:T(8,128)}, u32[]{:S(2)}) %copy-start.1) | copy-done | bytes 196632
  1.9 0.0 copy-start.2
  1.9 0.9 %copy-done.2 = s32[3,8,16,128]{3,2,1,0:T(8,128)S(1)} copy-done((s32[3,8,16,128]{3,2,1,0:T(8,128)S(1)}, s32[3,8,16,128]{3,2,1,0:T(8,128)}, u32[]{:S(2)}) %copy-start.2) | copy-done | bytes 196632
  2.8 0.0 copy-start.3
  2.8 0.8 %copy-done.3 = s32[8,16,128]{2,1,0:T(8,128)S(1)} copy-done((s32[8,16,128]{2,1,0:T(8,128)S(1)}, s32[8,16,128]{2,1,0:T(8,128)}, u32[]{:S(2)}) %copy-start.3) | copy-done | bytes 65560
  3.6 0.0 copy-start.4
  3.6 0.7 %copy-done.4 = f32[8]{0:T(128)S(1)} copy-done((f32[8]{0:T(128)S(1)}, f32[8]{0:T(128)}, u32[]{:S(2)}) %copy-start.4) | copy-done | bytes 56
  4.3 19.1 %shard_map.55 = f32[3,8,16,128]{3,2,1,0:T(8,128)S(1)} custom-call(f32[8]{0:T(128)S(1)} %copy-done.4, f32[3,8,16,128]{3,2,1,0:T(8,128)S(1)} %copy-done, f32[3,8,16,128]{3,2,1,0:T(8,128)S(1)} %copy-done.1, s32[8,16,128]{2,1,0:T(8,128)S(1)} %copy-done.3, s32[3,8,16,128]{3,2,1,0:T(8,128)S(1)} %copy-done.2), custom_call_target="tpu_custom_call" | custom-call | tf_op jit(solution)/shard_map/pallas_call | solution.py:395
  23.4 0.7 %copy.7 = f32[3,8,16,128]{3,2,1,0:T(8,128)} copy(f32[3,8,16,128]{3,2,1,0:T(8,128)S(1)} %shard_map.55) | data formatting | bytes 393216
Async XLA Ops:
  0.0 0.9 %copy-start = (f32[3,8,16,128]{3,2,1,0:T(8,128)S(1)}, f32[3,8,16,128]{3,2,1,0:T(8,128)}, u32[]{:S(2)}) copy-start(f32[3,8,16,128]{3,2,1,0:T(8,128)} %rhs_hbm.1) | copy-start | bytes 589828
  0.9 0.9 %copy-start.1 = (f32[3,8,16,128]{3,2,1,0:T(8,128)S(1)}, f32[3,8,16,128]{3,2,1,0:T(8,128)}, u32[]{:S(2)}) copy-start(f32[3,8,16,128]{3,2,1,0:T(8,128)} %frac_hbm.1) | copy-start | bytes 589828
  1.9 0.9 %copy-start.2 = (s32[3,8,16,128]{3,2,1,0:T(8,128)S(1)}, s32[3,8,16,128]{3,2,1,0:T(8,128)}, u32[]{:S(2)}) copy-start(s32[3,8,16,128]{3,2,1,0:T(8,128)} %flag_hbm.1) | copy-start | bytes 589828
  2.8 0.8 %copy-start.3 = (s32[8,16,128]{2,1,0:T(8,128)S(1)}, s32[8,16,128]{2,1,0:T(8,128)}, u32[]{:S(2)}) copy-start(s32[8,16,128]{2,1,0:T(8,128)} %reg_hbm.1) | copy-start | bytes 196612
  3.6 0.7 %copy-start.4 = (f32[8]{0:T(128)S(1)}, f32[8]{0:T(128)}, u32[]{:S(2)}) copy-start(f32[8]{0:T(128)} %cond.1) | copy-start | bytes 100

commit v3 on v2

--- a/solution.py
+++ b/solution.py
@@ -108,7 +108,6 @@
         return {axis: lax.rem(pos[axis] + (step + size[axis]), size[axis]) for axis, step in steps.items()}
 
     partners = [device(gx=1), device(gx=-1), device(gz=1), device(gz=-1), device(gy=1)]
-    partners += [device(gx=i, gz=j) for i in (1, -1) for j in (1, -1)]
     if gy > 2:
         partners.append(device(gy=-1))
     barrier = pltpu.get_barrier_semaphore()
@@ -137,7 +136,6 @@
 
     packs = [[None] * tiles for _ in range(6)]
     outer = {nx - 3: 0, 3: 1}
-    sent_first = {}
     for x in range(nx):
         region = reg_ref[x]
         sigma = jnp.zeros((ny, nz), jnp.float32)
@@ -153,26 +151,10 @@
                 old = packs[f][t]
                 packs[f][t] = piece if old is None else jnp.where(slot == j, piece, old)
             if x in outer:
-                first = start_iter(rhs, ks)
-                kf[outer[x], k] = first
-                sent_first[outer[x], k] = end_piece(first, j)
+                kf[outer[x], k] = start_iter(rhs, ks)
     for f in range(6):
         for t in range(tiles):
             w[f, t] = packs[f][t]
-    for side in range(2):
-        mine = (lane >= half) if side == 0 else low_half
-        j = (nx - 3) % per if side == 0 else 3
-        for zside, off in ((0, 8), (1, 4)):
-            tile = None
-            for f in range(6):
-                v = packs[f][tiles - 1 if side == 0 else 0]
-                if f < 3:
-                    v = jnp.where(slot == j, sent_first[side, f], v)
-                moved = rot(v, 4 * (f % 4) - off + (half if f >= 4 else 0), 1)
-                where = (quad == f % 4) & (mine if f < 4 else ~mine)
-                tile = moved if tile is None else jnp.where(where, moved, tile)
-            ds[side, zside] = tile
-
     pl.semaphore_wait(barrier, len(partners))
 
     def copy(number, src, dst, where):
@@ -186,10 +168,6 @@
     own_rows = pl.ds(0, ny)
     z_copies = [copy(0, w, wz.at[0], device(gz=1)), copy(1, w, wz.at[1], device(gz=-1))]
     x_copies = [
-        copy(2 + 2 * side + zside, ds.at[side, zside], dr.at[side, zside], device(gx=1 - 2 * side, gz=2 * zside - 1))
-        for side in range(2) for zside in range(2)
-    ]
-    x_copies += [
         copy(6, e.at[:, pl.ds(PAD + nx - 2, 2), own_rows], e.at[:, pl.ds(2, 2), own_rows], device(gx=1)),
         copy(7, e.at[:, pl.ds(PAD, 3), own_rows], e.at[:, pl.ds(PAD + nx, 3), own_rows], device(gx=-1)),
         copy(8, kf.at[0], e.at[pl.ds(0, 3), 1, own_rows], device(gx=1)),
@@ -254,17 +232,32 @@
     y_own = y_start(10, own, ya, yra)
     y_finish(y_own, own, yra)
     first_range(own)
-    curl_sweep(u1, PAD + 1, PAD + nx - 1, emit_second)
-    curl_sweep(u2, PAD + 2, PAD + nx - 2, emit_masked)
-    node_range(PAD + 3, PAD + nx - 2)
-
     for one in z_copies:
         one.wait()
+    for side in range(2):
+        mine = (lane >= half) if side == 0 else low_half
+        j = (nx - 3) % per if side == 0 else 3
+        t = tiles - 1 if side == 0 else 0
+        for zside, off in ((0, 8), (1, 4)):
+            tile = None
+            for f in range(6):
+                v = wz[1 - zside, f, t]
+                if f < 3:
+                    v = jnp.where(slot == j, start_iter(v, wz[1 - zside, 3 + f, t]), v)
+                moved = rot(v, 4 * (f % 4) - off + (half if f >= 4 else 0), 1)
+                where = (quad == f % 4) & (mine if f < 4 else ~mine)
+                tile = moved if tile is None else jnp.where(where, moved, tile)
+            ds[side, zside] = tile
+    x_copies += [copy(2 + side, ds.at[side], dr.at[side], device(gx=1 - 2 * side)) for side in range(2)]
     for f in range(6):
         for t in range(tiles):
             mid = w[f, t]
             e[f, base_a + t, 0:ny, :] = jnp.where(left, mid, wz[1, f, t])
             e[f, base_b + t, 0:ny, :] = jnp.where(left, wz[0, f, t], mid)
+    curl_sweep(u1, PAD + 1, PAD + nx - 1, emit_second)
+    curl_sweep(u2, PAD + 2, PAD + nx - 2, emit_masked)
+    node_range(PAD + 3, PAD + nx - 2)
+
     for one in x_copies:
         one.wait()
     for f in range(6):
@@ -421,7 +414,7 @@
             pltpu.SemaphoreType.DMA((14,)),
         ],
         compiler_params=pltpu.CompilerParams(
-            collective_id=0, has_side_effects=True, vmem_limit_bytes=40 * 1024 * 1024
+            collective_id=0, has_side_effects=True, vmem_limit_bytes=60 * 1024 * 1024
         ),
     )(conductivity, rhs, fraction, region, flags)
 

time: 24.3 us -> 20.1 us (0.83)
  local copies, waits for them, and re-layouts: 4.95 us -> 0.68 us
    unnamed x11 -> x1, local copies, waits for them, and re-layouts: 4.95 us -> 0.68 us
where the time goes in v3:
time: 20.1 us; the launch traced here: 19.9 us
  Pallas kernels  19.2 us (96%)
  local copies, waits for them, and re-layouts  0.68 us (3%)
    pallas_call x1, Pallas kernels, on_device(): pl.pallas_call(functools.partial(kernel, sizes, nx, ny, nz), out_shape=pl...  19.2 us
    unnamed x1, local copies, waits for them, and re-layouts  0.68 us

profile of v3, /device:TPU:0, one launch (start us, length us, event | category | flops | bytes accessed | tf_op | source)
XLA Modules:
  0.0 19.9 jit_solution(1218249245601605247)
XLA Ops:
  0.0 19.2 %shard_map.55 = f32[3,8,16,128]{3,2,1,0:T(8,128)S(1)} custom-call(f32[8]{0:T(128)} %cond.1, f32[3,8,16,128]{3,2,1,0:T(8,128)} %rhs_hbm.1, f32[3,8,16,128]{3,2,1,0:T(8,128)} %frac_hbm.1, s32[8,16,128]{2,1,0:T(8,128)} %reg_hbm.1, s32[3,8,16,128]{3,2,1,0:T(8,128)} %flag_hbm.1), custom_call_target="tpu_custom_call" | custom-call | tf_op jit(solution)/shard_map/pallas_call | solution.py:388
  19.2 0.7 %copy.7 = f32[3,8,16,128]{3,2,1,0:T(8,128)} copy(f32[3,8,16,128]{3,2,1,0:T(8,128)S(1)} %shard_map.55) | data formatting | bytes 393216
